TPU v7x, 32 devices: a whole 2x2x4 slice. The times are simulated.
32 devices in a mesh: dp: 8 (over y, x, core), tensor: 4 (over z).
Axes of the slice: x: 2, y: 2, z: 4, core: 2. Of those that a mesh axis runs over, the one named last changes fastest.
Arguments:
- activations: bfloat16 [8, 1024, 1536], P('dp', 'tensor'), may hold values from -6 to 6
- lengths: int32 [8], P('dp'), may hold values from 256 to 1024, as said below
- attn_gain: bfloat16 [1536], P('dp'), may hold values from 0.5 to 1.5
- w_query: bfloat16 [1536, 1536], P('dp', 'tensor'), may hold values from -0.15625 to 0.15625
- w_key: bfloat16 [1536, 768], P('dp', 'tensor'), may hold values from -0.15625 to 0.15625
- w_value: bfloat16 [1536, 768], P('dp', 'tensor'), may hold values from -0.15625 to 0.15625
- w_out: bfloat16 [1536, 1536], P('tensor', 'dp'), may hold values from -3 to 3
- mlp_gain: bfloat16 [1536], P('dp'), may hold values from 0.5 to 1.5
- w_gate: bfloat16 [1536, 4096], P('dp', 'tensor'), may hold values from -0.15625 to 0.15625
- w_up: bfloat16 [1536, 4096], P('dp', 'tensor'), may hold values from -0.15625 to 0.15625
- w_down: bfloat16 [4096, 1536], P('tensor', 'dp'), may hold values from -0.09375 to 0.09375
- cotangent: bfloat16 [8, 1024, 1536], P('dp', 'tensor'), may hold values from -6 to 6
Outputs:
- out_acts: float32 [8, 1024, 1536], P('dp', 'tensor')
- grad_acts: float32 [8, 1024, 1536], P('dp', 'tensor')
- grad_attn_gain: float32 [1536], P('dp')
- grad_query: float32 [1536, 1536], P('dp', 'tensor')
- grad_key: float32 [1536, 768], P('dp', 'tensor')
- grad_value: float32 [1536, 768], P('dp', 'tensor')
- grad_out: float32 [1536, 1536], P('tensor', 'dp')
- grad_mlp_gain: float32 [1536], P('dp')
- grad_gate: float32 [1536, 4096], P('dp', 'tensor')
- grad_up: float32 [1536, 4096], P('dp', 'tensor')
- grad_down: float32 [4096, 1536], P('tensor', 'dp')
Inputs may be any that keep to these rules, and one draw needn't show every extreme that they name: `lengths`: valid slots of each sequence; in every draw one sequence is full (1024) and one has exactly 256.
All inputs are finite; a program needn't handle non-finite values.
Results may differ from a plain program's by a relative error of at most 0.017.
Values may be sent and summed in bfloat16 or wider, within the bound.
A program may use at most 192 MiB of HBM per device.

v0:
```python
import math
import jax
import jax.numpy as jnp
from jax import lax
from jax.sharding import PartitionSpec as P

HEAD_DIM = 96
EPS = 1e-05
THETA = 100000.0
NEG = -1e30


def rope_tables(count, width):
    half = width // 2
    freqs = THETA ** (-jnp.arange(half, dtype=jnp.float32) * (2.0 / width))
    angles = jnp.arange(count, dtype=jnp.float32)[:, None] * freqs[None, :]
    return (jnp.cos(angles), jnp.sin(angles))


def rotate(vectors, cosines, sines):
    half = vectors.shape[-1] // 2
    first = vectors[..., :half]
    second = vectors[..., half:]
    cos_b = cosines[:, None, :]
    sin_b = sines[:, None, :]
    return jnp.concatenate(
        [first * cos_b - second * sin_b, second * cos_b + first * sin_b], axis=-1
    )


def unrotate(grads, cosines, sines):
    half = grads.shape[-1] // 2
    first = grads[..., :half]
    second = grads[..., half:]
    cos_b = cosines[:, None, :]
    sin_b = sines[:, None, :]
    return jnp.concatenate(
        [first * cos_b + second * sin_b, second * cos_b - first * sin_b], axis=-1
    )


def transposed(left, right):
    return lax.dot_general(
        left, right, (((1,), (1,)), ((), ())), preferred_element_type=jnp.float32
    )


def outer_sum(left, right):
    return lax.dot_general(
        left, right, (((0,), (0,)), ((), ())), preferred_element_type=jnp.float32
    )


def rms_back(grad_norm, normed, inverse):
    return inverse * (grad_norm - normed * jnp.mean(grad_norm * normed, axis=1, keepdims=True))


def scores_block(query_block, key_prefix, start, seq_positions, key_valid, scale):
    block = query_block.shape[0]
    stop = key_prefix.shape[0]
    raw = (
        jnp.einsum("qcgd,kcd->cgqk", query_block, key_prefix, preferred_element_type=jnp.float32)
        * scale
    )
    rows = start + jnp.arange(block)
    allowed = (seq_positions[None, :stop] <= rows[:, None]) & key_valid[None, :stop]
    return jnp.where(allowed, raw, NEG)


def body(
    activations,
    lengths,
    attn_gain,
    w_query,
    w_key,
    w_value,
    w_out,
    mlp_gain,
    w_gate,
    w_up,
    w_down,
    cotangent,
):
    tensor_size = lax.axis_size("tensor")
    tensor_rank = lax.axis_index("tensor")
    tokens = activations[0].astype(jnp.float32)
    local = tokens.shape[0]
    seq_len = local * tensor_size
    length = lengths[0]
    own_valid = (tensor_rank * local + jnp.arange(local) < length)[:, None]
    seq_positions = jnp.arange(seq_len)
    key_valid = seq_positions < length
    cosines, sines = rope_tables(seq_len, HEAD_DIM)
    scale = 1.0 / math.sqrt(HEAD_DIM)
    query_full, key_full, value_full, out_full, first_gain = (
        lax.all_gather(w_query, "dp", axis=0, tiled=True),
        lax.all_gather(w_key, "dp", axis=0, tiled=True),
        lax.all_gather(w_value, "dp", axis=0, tiled=True),
        lax.all_gather(w_out, "dp", axis=1, tiled=True),
        lax.all_gather(attn_gain, "dp", axis=0, tiled=True),
    )
    heads = query_full.shape[1] // HEAD_DIM
    kv_local = key_full.shape[1] // HEAD_DIM
    groups = heads // kv_local
    first_gain_f = first_gain.astype(jnp.float32)
    inv_first = lax.rsqrt(jnp.mean(tokens * tokens, axis=1, keepdims=True) + EPS)
    normed_first = tokens * inv_first
    first_low = (normed_first * first_gain_f).astype(jnp.bfloat16)
    first_all = lax.all_gather(first_low, "tensor", axis=0, tiled=True)
    query_proj = jnp.dot(first_all, query_full, preferred_element_type=jnp.float32).reshape(
        seq_len, heads, HEAD_DIM
    )
    queries = (
        rotate(query_proj, cosines, sines)
        .astype(jnp.bfloat16)
        .reshape(seq_len, kv_local, groups, HEAD_DIM)
    )
    key_proj = jnp.dot(first_all, key_full, preferred_element_type=jnp.float32).reshape(
        seq_len, kv_local, HEAD_DIM
    )
    keys = rotate(key_proj, cosines, sines).astype(jnp.bfloat16)
    values = (
        jnp.dot(first_all, value_full, preferred_element_type=jnp.float32)
        .astype(jnp.bfloat16)
        .reshape(seq_len, kv_local, HEAD_DIM)
    )
    block = min(512, seq_len)
    count = seq_len // block
    pieces = []
    log_sums = []
    for index in range(count):
        start = index * block
        stop = start + block
        scores = scores_block(
            queries[start:stop], keys[:stop], start, seq_positions, key_valid, scale
        )
        peak = jnp.max(scores, axis=3, keepdims=True)
        log_sum = peak + jnp.log(jnp.sum(jnp.exp(scores - peak), axis=3, keepdims=True))
        probs = jnp.exp(scores - log_sum)
        mixed = jnp.einsum(
            "cgqk,kcd->qcgd",
            probs.astype(jnp.bfloat16),
            values[:stop],
            preferred_element_type=jnp.float32,
        )
        pieces.append(mixed.reshape(block, heads * HEAD_DIM))
        log_sums.append(log_sum)
    attended = jnp.concatenate(pieces, axis=0).astype(jnp.bfloat16)
    branch = lax.psum_scatter(
        jnp.dot(attended, out_full, preferred_element_type=jnp.float32),
        "tensor",
        scatter_dimension=0,
        tiled=True,
    )
    middle = tokens + branch
    gate_full, up_full, down_full, second_gain = (
        lax.all_gather(w_gate, "dp", axis=0, tiled=True),
        lax.all_gather(w_up, "dp", axis=0, tiled=True),
        lax.all_gather(w_down, "dp", axis=1, tiled=True),
        lax.all_gather(mlp_gain, "dp", axis=0, tiled=True),
    )
    second_gain_f = second_gain.astype(jnp.float32)
    inv_second = lax.rsqrt(jnp.mean(middle * middle, axis=1, keepdims=True) + EPS)
    normed_second = middle * inv_second
    second_low = (normed_second * second_gain_f).astype(jnp.bfloat16)
    second_all = lax.all_gather(second_low, "tensor", axis=0, tiled=True)
    gate = jnp.dot(second_all, gate_full, preferred_element_type=jnp.float32)
    up_part = jnp.dot(second_all, up_full, preferred_element_type=jnp.float32)
    sigmoid_gate = jax.nn.sigmoid(gate)
    hidden = (gate * sigmoid_gate * up_part).astype(jnp.bfloat16)
    result = middle + lax.psum_scatter(
        jnp.dot(hidden, down_full, preferred_element_type=jnp.float32).astype(jnp.bfloat16),
        "tensor",
        scatter_dimension=0,
        tiled=True,
    ).astype(jnp.float32)
    output = jnp.where(own_valid, result, 0.0)
    query_full, key_full, value_full, out_full, gate_full, up_full, down_full = (
        lax.all_gather(w_query, "dp", axis=0, tiled=True),
        lax.all_gather(w_key, "dp", axis=0, tiled=True),
        lax.all_gather(w_value, "dp", axis=0, tiled=True),
        lax.all_gather(w_out, "dp", axis=1, tiled=True),
        lax.all_gather(w_gate, "dp", axis=0, tiled=True),
        lax.all_gather(w_up, "dp", axis=0, tiled=True),
        lax.all_gather(w_down, "dp", axis=1, tiled=True),
    )
    grad_result = jnp.where(own_valid, cotangent[0].astype(jnp.float32), 0.0)
    grad_mlp_all = lax.all_gather(grad_result.astype(jnp.bfloat16), "tensor", axis=0, tiled=True)
    grad_down_w = outer_sum(hidden, grad_mlp_all)
    grad_hidden = transposed(grad_mlp_all, down_full)
    grad_gate_low = (
        grad_hidden * up_part * sigmoid_gate * (1.0 + gate * (1.0 - sigmoid_gate))
    ).astype(jnp.bfloat16)
    grad_up_low = (grad_hidden * gate * sigmoid_gate).astype(jnp.bfloat16)
    grad_second = lax.psum_scatter(
        transposed(grad_gate_low, gate_full) + transposed(grad_up_low, up_full),
        "tensor",
        scatter_dimension=0,
        tiled=True,
    )
    grad_gate_w = outer_sum(second_all, grad_gate_low)
    grad_up_w = outer_sum(second_all, grad_up_low)
    grad_gate_w, grad_up_w, grad_down_w = (
        lax.psum_scatter(
            grad_gate_w.astype(jnp.bfloat16), "dp", scatter_dimension=0, tiled=True
        ).astype(jnp.float32),
        lax.psum_scatter(
            grad_up_w.astype(jnp.bfloat16), "dp", scatter_dimension=0, tiled=True
        ).astype(jnp.float32),
        lax.psum_scatter(
            grad_down_w.astype(jnp.bfloat16), "dp", scatter_dimension=1, tiled=True
        ).astype(jnp.float32),
    )
    second_gain_part = jnp.sum(grad_second * normed_second, axis=0)
    grad_middle = grad_result + rms_back(grad_second * second_gain_f, normed_second, inv_second)
    grad_attn_all = lax.all_gather(grad_middle.astype(jnp.bfloat16), "tensor", axis=0, tiled=True)
    grad_attended = transposed(grad_attn_all, out_full).astype(jnp.bfloat16)
    grad_out_w = outer_sum(attended, grad_attn_all)
    grad_queries = []
    grad_keys = jnp.zeros((seq_len, kv_local, HEAD_DIM), jnp.float32)
    grad_values = jnp.zeros((seq_len, kv_local, HEAD_DIM), jnp.float32)
    for index in range(count):
        start = index * block
        stop = start + block
        query_block = queries[start:stop]
        scores = scores_block(query_block, keys[:stop], start, seq_positions, key_valid, scale)
        probs = jnp.exp(scores - log_sums[index])
        grad_block = grad_attended[start:stop].reshape(block, kv_local, groups, HEAD_DIM)
        grad_probs = jnp.einsum(
            "qcgd,kcd->cgqk", grad_block, values[:stop], preferred_element_type=jnp.float32
        )
        row_dot = jnp.sum(probs * grad_probs, axis=3, keepdims=True)
        grad_scores = (probs * (grad_probs - row_dot)).astype(jnp.bfloat16)
        query_grad = (
            jnp.einsum(
                "cgqk,kcd->qcgd", grad_scores, keys[:stop], preferred_element_type=jnp.float32
            )
            * scale
        )
        grad_queries.append(query_grad.reshape(block, heads, HEAD_DIM))
        key_grad = (
            jnp.einsum(
                "cgqk,qcgd->kcd", grad_scores, query_block, preferred_element_type=jnp.float32
            )
            * scale
        )
        grad_keys = grad_keys.at[:stop].add(key_grad)
        value_grad = jnp.einsum(
            "cgqk,qcgd->kcd",
            probs.astype(jnp.bfloat16),
            grad_block,
            preferred_element_type=jnp.float32,
        )
        grad_values = grad_values.at[:stop].add(value_grad)
    grad_query_proj = (
        unrotate(jnp.concatenate(grad_queries, axis=0), cosines, sines)
        .astype(jnp.bfloat16)
        .reshape(seq_len, heads * HEAD_DIM)
    )
    grad_key_proj = (
        unrotate(grad_keys, cosines, sines)
        .astype(jnp.bfloat16)
        .reshape(seq_len, kv_local * HEAD_DIM)
    )
    grad_value_proj = grad_values.astype(jnp.bfloat16).reshape(seq_len, kv_local * HEAD_DIM)
    grad_first = lax.psum_scatter(
        (
            transposed(grad_query_proj, query_full)
            + transposed(grad_key_proj, key_full)
            + transposed(grad_value_proj, value_full)
        ).astype(jnp.bfloat16),
        "tensor",
        scatter_dimension=0,
        tiled=True,
    ).astype(jnp.float32)
    grad_query_w = outer_sum(first_all, grad_query_proj)
    grad_key_w = outer_sum(first_all, grad_key_proj)
    grad_value_w = outer_sum(first_all, grad_value_proj)
    grad_query_w, grad_key_w, grad_value_w, grad_out_w = (
        lax.psum_scatter(
            grad_query_w.astype(jnp.bfloat16), "dp", scatter_dimension=0, tiled=True
        ).astype(jnp.float32),
        lax.psum_scatter(
            grad_key_w.astype(jnp.bfloat16), "dp", scatter_dimension=0, tiled=True
        ).astype(jnp.float32),
        lax.psum_scatter(
            grad_value_w.astype(jnp.bfloat16), "dp", scatter_dimension=0, tiled=True
        ).astype(jnp.float32),
        lax.psum_scatter(
            grad_out_w.astype(jnp.bfloat16), "dp", scatter_dimension=1, tiled=True
        ).astype(jnp.float32),
    )
    first_gain_part = jnp.sum(grad_first * normed_first, axis=0)
    grad_tokens = grad_middle + rms_back(grad_first * first_gain_f, normed_first, inv_first)
    first_gain_sum, second_gain_sum = lax.psum(
        (first_gain_part, second_gain_part), ("dp", "tensor")
    )
    width = attn_gain.shape[0]
    dp_rank = lax.axis_index("dp")
    first_gain_grad = lax.dynamic_slice_in_dim(first_gain_sum, dp_rank * width, width)
    second_gain_grad = lax.dynamic_slice_in_dim(second_gain_sum, dp_rank * width, width)
    return (
        output[None],
        grad_tokens[None],
        first_gain_grad,
        grad_query_w,
        grad_key_w,
        grad_value_w,
        grad_out_w,
        second_gain_grad,
        grad_gate_w,
        grad_up_w,
        grad_down_w,
    )


def solution(mesh):
    return jax.shard_map(
        body,
        mesh=mesh,
        in_specs=(
            P("dp", "tensor", None),
            P("dp"),
            P("dp"),
            P("dp", "tensor"),
            P("dp", "tensor"),
            P("dp", "tensor"),
            P("tensor", "dp"),
            P("dp"),
            P("dp", "tensor"),
            P("dp", "tensor"),
            P("tensor", "dp"),
            P("dp", "tensor", None),
        ),
        out_specs=(
            P("dp", "tensor", None),
            P("dp", "tensor", None),
            P("dp"),
            P("dp", "tensor"),
            P("dp", "tensor"),
            P("dp", "tensor"),
            P("tensor", "dp"),
            P("dp"),
            P("dp", "tensor"),
            P("dp", "tensor"),
            P("tensor", "dp"),
        ),
        check_vma=False,
    )
```

profile of v0, /device:TPU:0, one launch (start us, length us, event | category | flops | bytes accessed | tf_op | source)
XLA Modules:
  0.0 1172.5 jit_solution(16675903397976520684)
XLA Ops:
  12.3 15.5 %all-reduce.5 = (bf16[1536]{0:T(1024)(128)(2,1)S(1)}, bf16[1536]{0:T(1024)(128)(2,1)S(1)}) all-reduce(bf16[1536]{0:T(1024)(128)(2,1)S(1)} %dynamic-update-slice.10, bf16[1536]{0:T(1024)(128)(2,1)S(1)} %dynamic-update-slice.11), channel_id=1, replica_groups=mesh['dp'=8,'tensor'=4] {'dp'}, use_global_device_ids=true, to_apply=%add.2 | all-reduce | flops 3072 | bytes 12288
  33.5 9.4 all_gather.49
  42.9 10.4 all_gather.48
  53.6 39.4 %all-gather.10.cloned.1.call-done = bf16[1024,1536]{1,0:T(8,128)(2,1)} async-done(((bf16[256,1536]{1,0:T(8,128)(2,1)}), bf16[1024,1536]{1,0:T(8,128)(2,1)}) %all-gather.10.cloned.1.call-update) | async-done | bytes 3145744 | tf_op jit(solution)/shard_map/all_gather | solution.py:109
  98.4 19.2 %all-gather.12.cloned.1.call-done = bf16[1536,384]{1,0:T(8,128)(2,1)} async-done(((bf16[192,384]{1,0:T(8,128)(2,1)}), bf16[1536,384]{1,0:T(8,128)(2,1)}) %all-gather.12.cloned.1.call-update) | async-done | bytes 1179664 | tf_op jit(solution)/shard_map/all_gather | solution.py:96
  132.0 11.4 all-gather.14.cloned.1.call-done
  149.8 110.3 %reduce-scatter.12.cloned.1.call-done = f32[256,1536]{1,0:T(8,128)} async-done(((f32[1024,1536]{1,0:T(8,128)}), f32[256,1536]{1,0:T(8,128)}) %reduce-scatter.12.cloned.1.call-update) | async-done | bytes 1572880 | tf_op jit(solution)/shard_map/reduce_scatter | solution.py:149
  267.3 27.3 %all-gather.20.cloned.1.call-done = bf16[1536,1024]{1,0:T(8,128)(2,1)} async-done(((bf16[192,1024]{1,0:T(8,128)(2,1)}), bf16[1536,1024]{1,0:T(8,128)(2,1)}) %all-gather.20.cloned.1.call-update) | async-done | bytes 3145744 | tf_op jit(solution)/shard_map/all_gather | solution.py:158
  294.6 65.5 %all-gather.16.cloned.1.call-done = bf16[1024,1536]{1,0:T(8,128)(2,1)} async-done(((bf16[256,1536]{1,0:T(8,128)(2,1)}), bf16[1024,1536]{1,0:T(8,128)(2,1)}) %all-gather.16.cloned.1.call-update) | async-done | bytes 3145744 | tf_op jit(solution)/shard_map/all_gather | solution.py:166
  360.1 8.2 fusion.63
  368.3 24.5 %all-gather.18.cloned.1.call-done = bf16[1536,1024]{1,0:T(8,128)(2,1)} async-done(((bf16[192,1024]{1,0:T(8,128)(2,1)}), bf16[1536,1024]{1,0:T(8,128)(2,1)}) %all-gather.18.cloned.1.call-update) | async-done | bytes 3145744 | tf_op jit(solution)/shard_map/all_gather | solution.py:157
  392.8 8.2 fusion.62
  401.1 57.4 %all-gather.24.cloned.1.call-done = bf16[1024,1536]{1,0:T(8,128)(2,1)} async-done(((bf16[256,1536]{1,0:T(8,128)(2,1)}), bf16[1024,1536]{1,0:T(8,128)(2,1)}) %all-gather.24.cloned.1.call-update) | async-done | bytes 3145744 | tf_op jit(solution)/shard_map/all_gather | solution.py:188
  458.4 32.7 %all-gather.22.cloned.1.call-done = bf16[1024,1536]{0,1:T(8,128)(2,1)} async-done(((bf16[1024,192]{0,1:T(8,128)(2,1)}), bf16[1024,1536]{0,1:T(8,128)(2,1)}) %all-gather.22.cloned.1.call-update) | async-done | bytes 3145744 | tf_op jit(solution)/shard_map/all_gather | solution.py:159
  491.2 11.7 %multiply_convert_fusion = (bf16[1024,1024]{1,0:T(8,128)(2,1)S(1)}, bf16[1024,1024]{1,0:T(8,128)(2,1)S(1)}, bf16[1024,1024]{1,0:T(8,128)(2,1)}) fusion(f32[1024,1024]{1,0:T(8,128)} %fusion.62, f32[1024,1024]{1,0:T(8,128)} %fusion.63, bf16[1024,1536]{1,0:T(8,128)(2,1)} %all-gather.24.cloned.1.call-done, bf16[1024,1536]{0,1:T(8,128)(2,1)} %all-gather.22.cloned.1.call-done), kind=kOutput, calls=%fused_computation.18 | convolution fusion | flops 3238002688 | bytes 20971520 | tf_op jit(solution)/shard_map/dot_general | solution.py:43
  512.2 7.7 convolution_convert_fusion.3
  519.9 103.1 %reduce-scatter.16.cloned.1.call-done = f32[256,1536]{1,0:T(8,128)} async-done(((f32[1024,1536]{1,0:T(8,128)}), f32[256,1536]{1,0:T(8,128)}) %reduce-scatter.16.cloned.1.call-update) | async-done | bytes 1572880 | tf_op jit(solution)/shard_map/reduce_scatter | solution.py:195
  624.9 61.4 %reduce-scatter.14.cloned.1.call-done = bf16[256,1536]{1,0:T(8,128)(2,1)} async-done(((bf16[1024,1536]{1,0:T(8,128)(2,1)}), bf16[256,1536]{1,0:T(8,128)(2,1)}) %reduce-scatter.14.cloned.1.call-update) | async-done | bytes 786448 | tf_op jit(solution)/shard_map/reduce_scatter | solution.py:171
  690.8 7.6 convolution_convert_fusion
  698.5 8.0 convolution_convert_fusion.1
  706.6 7.7 convolution_convert_fusion.2
  714.6 39.7 %all-gather.26.cloned.1.call-done = bf16[1024,1536]{1,0:T(8,128)(2,1)} async-done(((bf16[256,1536]{1,0:T(8,128)(2,1)}), bf16[1024,1536]{1,0:T(8,128)(2,1)}) %all-gather.26.cloned.1.call-update) | async-done | bytes 3145744 | tf_op jit(solution)/shard_map/all_gather | solution.py:216
  770.0 9.5 fusion
  780.0 7.1 fusion.2
  815.7 36.0 %reduce-scatter.30.cloned.1.call-done = bf16[192,1024]{1,0:T(8,128)(2,1)} async-done(((bf16[1536,1024]{1,0:T(8,128)(2,1)}), bf16[192,1024]{1,0:T(8,128)(2,1)}) %reduce-scatter.30.cloned.1.call-update) | async-done | bytes 393232 | tf_op jit(solution)/shard_map/reduce_scatter | solution.py:207
  853.7 47.4 %reduce-scatter.28.cloned.1.call-done = bf16[192,1024]{1,0:T(8,128)(2,1)} async-done(((bf16[1536,1024]{1,0:T(8,128)(2,1)}), bf16[192,1024]{1,0:T(8,128)(2,1)}) %reduce-scatter.28.cloned.1.call-update) | async-done | bytes 393232 | tf_op jit(solution)/shard_map/reduce_scatter | solution.py:204
  903.1 36.0 %reduce-scatter.24.cloned.1.call-done = bf16[192,192]{1,0:T(8,128)(2,1)} async-done(((bf16[1536,192]{1,0:T(8,128)(2,1)}), bf16[192,192]{1,0:T(8,128)(2,1)}) %reduce-scatter.24.cloned.1.call-update) | async-done | bytes 73744 | tf_op jit(solution)/shard_map/reduce_scatter | solution.py:286
  940.7 36.4 %reduce-scatter.22.cloned.1.call-done = bf16[192,192]{1,0:T(8,128)(2,1)} async-done(((bf16[1536,192]{1,0:T(8,128)(2,1)}), bf16[192,192]{1,0:T(8,128)(2,1)}) %reduce-scatter.22.cloned.1.call-update) | async-done | bytes 73744 | tf_op jit(solution)/shard_map/reduce_scatter | solution.py:283
  978.6 38.2 %reduce-scatter.26.cloned.1.call-done = bf16[384,192]{0,1:T(8,128)(2,1)} async-done(((bf16[384,1536]{0,1:T(8,128)(2,1)}), bf16[384,192]{0,1:T(8,128)(2,1)}) %reduce-scatter.26.cloned.1.call-update) | async-done | bytes 147472 | tf_op jit(solution)/shard_map/reduce_scatter | solution.py:289
  1018.5 38.3 %reduce-scatter.20.cloned.1.call-done = bf16[192,384]{1,0:T(8,128)(2,1)} async-done(((bf16[1536,384]{1,0:T(8,128)(2,1)}), bf16[192,384]{1,0:T(8,128)(2,1)}) %reduce-scatter.20.cloned.1.call-update) | async-done | bytes 147472 | tf_op jit(solution)/shard_map/reduce_scatter | solution.py:280
  1058.5 60.9 %reduce-scatter.18.cloned.1.call-done = bf16[256,1536]{1,0:T(8,128)(2,1)} async-done(((bf16[1024,1536]{1,0:T(8,128)(2,1)}), bf16[256,1536]{1,0:T(8,128)(2,1)}) %reduce-scatter.18.cloned.1.call-update) | async-done | bytes 786448 | tf_op jit(solution)/shard_map/reduce_scatter | solution.py:266
  1121.2 40.3 %all-reduce.4 = (f32[1536]{0:T(1024)S(1)}, f32[1536]{0:T(1024)S(1)}) all-reduce(f32[1536]{0:T(1024)S(1)} %get-tuple-element.77, f32[1536]{0:T(1024)S(1)} %get-tuple-element.75), channel_id=1, replica_groups=mesh['dp'=8,'tensor'=4] {'dp','tensor'}, use_global_device_ids=true, to_apply=%region_15.16 | all-reduce | flops 3072 | bytes 24576 | tf_op jit(solution)/shard_map/psum | solution.py:295
  (224 shorter events, 119.3 us)
Async XLA Ops:
  7.2 35.7 %copy-start.43 = (bf16[192,192]{1,0:T(8,128)(2,1)S(1)}, bf16[192,192]{1,0:T(8,128)(2,1)}, u32[]{:S(2)}) copy-start(bf16[192,192]{1,0:T(8,128)(2,1)} %param.29) | copy-start | bytes 221188
  7.2 85.8 %all-gather.10.cloned.1.call-start = ((), (), s32[]{:S(2)}) async-start(), calls=%async_computation.11 | async-start | bytes 3932160 | tf_op jit(solution)/shard_map/all_gather | solution.py:109
  30.1 87.4 %all-gather.12.cloned.1.call-start = ((), (), s32[]{:S(2)}) async-start(), calls=%async_computation.12 | async-start | bytes 1327104 | tf_op jit(solution)/shard_map/all_gather | solution.py:96
  30.8 112.5 %all-gather.14.cloned.1.call-start = ((), (), s32[]{:S(2)}) async-start(), calls=%async_computation.13 | async-start | bytes 1327104 | tf_op jit(solution)/shard_map/all_gather | solution.py:99
  31.6 228.6 %reduce-scatter.12.cloned.1.call-start = ((), (), s32[]{:S(2)}) async-start(), calls=%async_computation.14 | async-start | bytes 7864320 | tf_op jit(solution)/shard_map/reduce_scatter | solution.py:149
  33.1 88.1 %copy-start.16 = (f32[1024,48]{0,1:T(8,128)}, f32[1024,48]{0,1:T(8,128)S(1)}, u32[]{:S(2)}) copy-start(f32[1024,48]{0,1:T(8,128)S(1)} %get-tuple-element.103) | copy-start | bytes 589828
  33.1 88.1 %copy-start.18 = (f32[1024,48]{0,1:T(8,128)}, f32[1024,48]{0,1:T(8,128)S(1)}, u32[]{:S(2)}) copy-start(f32[1024,48]{0,1:T(8,128)S(1)} %get-tuple-element.104) | copy-start | bytes 589828
  42.9 55.3 %copy-start.11 = (bf16[1536,192]{1,0:T(8,128)(2,1)}, bf16[1536,192]{1,0:T(8,128)(2,1)S(1)}, u32[]{:S(2)}) copy-start(bf16[1536,192]{1,0:T(8,128)(2,1)S(1)} %all_gather.49) | copy-start | bytes 1769476
  53.3 44.9 %copy-start.9 = (bf16[1536,192]{1,0:T(8,128)(2,1)}, bf16[1536,192]{1,0:T(8,128)(2,1)S(1)}, u32[]{:S(2)}) copy-start(bf16[1536,192]{1,0:T(8,128)(2,1)S(1)} %all_gather.48) | copy-start | bytes 1769476
  53.6 704.3 %copy-start.13 = (pred[512,512]{0,1:T(8,128)(4,1)}, pred[512,512]{0,1:T(8,128)(4,1)S(1)}, u32[]{:S(2)}) copy-start(pred[512,512]{0,1:T(8,128)(4,1)S(1)} %fusion.32) | copy-start | bytes 786436
  96.3 33.2 %copy-start.20 = (bf16[1024,192]{0,1:T(8,128)(2,1)}, bf16[1024,192]{0,1:T(8,128)(2,1)S(1)}, u32[]{:S(2)}) copy-start(bf16[1024,192]{0,1:T(8,128)(2,1)S(1)} %convolution_convert_fusion.11) | copy-start | bytes 1179652
  149.2 111.0 %copy-start.4 = (bf16[1,256,1536]{2,1,0:T(8,128)(2,1)S(1)}, bf16[1,256,1536]{2,1,0:T(8,128)(2,1)}, u32[]{:S(2)}) copy-start(bf16[1,256,1536]{2,1,0:T(8,128)(2,1)} %param.24) | copy-start | bytes 2359300
  149.2 145.4 %all-gather.20.cloned.1.call-start = ((), (), s32[]{:S(2)}) async-start(), calls=%async_computation.17 | async-start | bytes 3538944 | tf_op jit(solution)/shard_map/all_gather | solution.py:158
  149.8 210.3 %all-gather.16.cloned.1.call-start = ((), (), s32[]{:S(2)}) async-start(), calls=%async_computation.15 | async-start | bytes 3932160 | tf_op jit(solution)/shard_map/all_gather | solution.py:166
  262.9 129.9 %all-gather.18.cloned.1.call-start = ((), (), s32[]{:S(2)}) async-start(), calls=%async_computation.16 | async-start | bytes 3538944 | tf_op jit(solution)/shard_map/all_gather | solution.py:157
  263.7 194.7 %all-gather.24.cloned.1.call-start = ((), (), s32[]{:S(2)}) async-start(), calls=%async_computation.20 | async-start | bytes 3932160 | tf_op jit(solution)/shard_map/all_gather | solution.py:188
  266.0 225.2 %all-gather.22.cloned.1.call-start = ((), (), s32[]{:S(2)}) async-start(), calls=%async_computation.18 | async-start | bytes 3538944 | tf_op jit(solution)/shard_map/all_gather | solution.py:159
  266.7 356.3 %reduce-scatter.16.cloned.1.call-start = ((), (), s32[]{:S(2)}) async-start(), calls=%async_computation.21 | async-start | bytes 7864320 | tf_op jit(solution)/shard_map/reduce_scatter | solution.py:195
  512.1 174.2 %reduce-scatter.14.cloned.1.call-start = ((), (), s32[]{:S(2)}) async-start(), calls=%async_computation.19 | async-start | bytes 3932160 | tf_op jit(solution)/shard_map/reduce_scatter | solution.py:171
  519.9 234.4 %all-gather.26.cloned.1.call-start = ((), (), s32[]{:S(2)}) async-start(), calls=%async_computation.22 | async-start | bytes 3932160 | tf_op jit(solution)/shard_map/all_gather | solution.py:216
  690.8 122.9 %reduce-scatter.32.cloned.1.call-start = ((), (), s32[]{:S(2)}) async-start(), calls=%async_computation.30 | async-start | bytes 3538944 | tf_op jit(solution)/shard_map/reduce_scatter | solution.py:210
  698.5 153.3 %reduce-scatter.30.cloned.1.call-start = ((), (), s32[]{:S(2)}) async-start(), calls=%async_computation.29 | async-start | bytes 3538944 | tf_op jit(solution)/shard_map/reduce_scatter | solution.py:207
  706.6 194.5 %reduce-scatter.28.cloned.1.call-start = ((), (), s32[]{:S(2)}) async-start(), calls=%async_computation.28 | async-start | bytes 3538944 | tf_op jit(solution)/shard_map/reduce_scatter | solution.py:204
  714.3 39.9 %copy-start.34 = (bf16[384,1536]{0,1:T(8,128)(2,1)S(1)}, bf16[384,1536]{0,1:T(8,128)(2,1)}, u32[]{:S(2)}) copy-start(bf16[384,1536]{0,1:T(8,128)(2,1)} %all-gather.14.cloned.1.call-done) | copy-start | bytes 3538948
  714.4 224.7 %reduce-scatter.24.cloned.1.call-start = ((), (), s32[]{:S(2)}) async-start(), calls=%async_computation.26 | async-start | bytes 884736 | tf_op jit(solution)/shard_map/reduce_scatter | solution.py:286
  779.5 197.5 %reduce-scatter.22.cloned.1.call-start = ((), (), s32[]{:S(2)}) async-start(), calls=%async_computation.25 | async-start | bytes 884736 | tf_op jit(solution)/shard_map/reduce_scatter | solution.py:283
  792.9 223.9 %reduce-scatter.26.cloned.1.call-start = ((), (), s32[]{:S(2)}) async-start(), calls=%async_computation.27 | async-start | bytes 1327104 | tf_op jit(solution)/shard_map/reduce_scatter | solution.py:289
  798.1 258.7 %reduce-scatter.20.cloned.1.call-start = ((), (), s32[]{:S(2)}) async-start(), calls=%async_computation.24 | async-start | bytes 1327104 | tf_op jit(solution)/shard_map/reduce_scatter | solution.py:280
  807.4 312.0 %reduce-scatter.18.cloned.1.call-start = ((), (), s32[]{:S(2)}) async-start(), calls=%async_computation.23 | async-start | bytes 3932160 | tf_op jit(solution)/shard_map/reduce_scatter | solution.py:266
  813.6 305.8 %copy-start.41 = (f32[1536]{0:T(1024)S(1)}, f32[1536]{0:T(1024)}, u32[]{:S(2)}) copy-start(f32[1536]{0:T(1024)} %copy-done.40) | copy-start | bytes 18436
  813.6 305.8 %copy-start.45 = (f32[256]{0:T(256)S(1)}, f32[256]{0:T(256)}, u32[]{:S(2)}) copy-start(f32[256]{0:T(256)} %copy-done.44) | copy-start | bytes 3076
  813.6 349.2 %copy-start.15 = (f32[256,1536]{1,0:T(8,128)S(1)}, f32[256,1536]{1,0:T(8,128)}, u32[]{:S(2)}) copy-start(f32[256,1536]{1,0:T(8,128)} %get-tuple-element.84) | copy-start | bytes 4718596
  (40 other events, 256.6 us)
Sparse Core Ops, SparseCore 0:
  30.2 62.7 all-gather.9
  94.9 22.5 all-gather.11
  119.4 23.9 all-gather.13
  149.3 110.7 reduce-scatter.11
  261.9 32.6 all-gather.19
  296.6 63.4 all-gather.15
  362.0 30.8 all-gather.17
  395.0 63.4 all-gather.23
  460.3 30.8 all-gather.21
  512.3 110.7 reduce-scatter.15
  625.4 60.8 reduce-scatter.13
  690.9 63.3 all-gather.25
  757.7 44.7 reduce-scatter.31
  805.7 46.0 reduce-scatter.29
  855.0 46.0 reduce-scatter.27
  904.1 34.9 reduce-scatter.23
  942.1 34.9 reduce-scatter.21
  980.1 36.6 reduce-scatter.25
  1020.1 36.6 reduce-scatter.19
  1059.0 60.3 reduce-scatter.17
where the time goes:
time: 1180 us; the launch traced here: 1170 us
  waiting for transfers between devices  889 us (75%)
  matrix products  132 us (11%)
  blocking collectives  75.5 us (6%)
  other arithmetic  46.9 us (4%)
  between operations  16.7 us (1%)
    reduce_scatter x1, waiting for transfers between devices, body(): lax.psum_scatter(jnp.dot(attended, out_full, preferred_element_type=jnp.f...  110 us
    reduce_scatter x1, waiting for transfers between devices, body(): lax.psum_scatter(transposed(grad_gate_low, gate_full) + transposed(grad_u...  103 us
    all_gather x1, waiting for transfers between devices, body(): second_all = lax.all_gather(second_low, 'tensor', axis=0, tiled=True)  65.5 us
    reduce_scatter x1, waiting for transfers between devices, body(): lax.psum_scatter(jnp.dot(hidden, down_full, preferred_element_type=jnp.fl...  61.4 us
    reduce_scatter x1, waiting for transfers between devices, body(): lax.psum_scatter((transposed(grad_query_proj, query_full) + transposed(gr...  60.9 us
    all_gather x1, waiting for transfers between devices, body(): lax.all_gather(grad_result.astype(jnp.bfloat16), 'tensor', axis=0, tiled=...  57.4 us
    reduce_scatter x1, waiting for transfers between devices, body(): lax.psum_scatter(grad_gate_w.astype(jnp.bfloat16), 'dp', scatter_dimensio...  47.4 us
    psum x1, blocking collectives, body(): lax.psum((first_gain_part, second_gain_part), ('dp', 'tensor'))  40.3 us
  transfers between devices with their start and end apart: 20, of which 19 were waited for; matrix products, arithmetic and copies ran while one was open for 12% of the time, Pallas kernels for 0%

commit v1 on v0

--- a/solution.py
+++ b/solution.py
@@ -185,7 +185,17 @@
         lax.all_gather(w_down, "dp", axis=1, tiled=True),
     )
     grad_result = jnp.where(own_valid, cotangent[0].astype(jnp.float32), 0.0)
-    grad_mlp_all = lax.all_gather(grad_result.astype(jnp.bfloat16), "tensor", axis=0, tiled=True)
+    shard = grad_result.astype(jnp.bfloat16)
+    ways = lax.axis_size("tensor")
+    up = [(d, (d + 1) % ways) for d in range(ways)]
+    down = [(d, (d - 1) % ways) for d in range(ways)]
+    earlier, later = ([shard], [shard])
+    for _ in range(ways // 2):
+        earlier.append(lax.ppermute(earlier[-1], "tensor", up))
+    for _ in range((ways - 1) // 2):
+        later.append(lax.ppermute(later[-1], "tensor", down))
+    line = jnp.concatenate([*earlier[::-1], *later[1:]], axis=0)
+    grad_mlp_all = jnp.roll(line, (lax.axis_index("tensor") - ways // 2) * shard.shape[0], axis=0)
     grad_down_w = outer_sum(hidden, grad_mlp_all)
     grad_hidden = transposed(grad_mlp_all, down_full)
     grad_gate_low = (

time: 1180 us -> 1130 us (0.958)
  waiting for transfers between devices: 889 us -> 820 us
  local copies, waits for them, and re-layouts: 10.6 us -> 23.1 us
    ppermute x0 -> x3, waiting for transfers between devices: none -> 78.1 us  [the longest x1 39.2 us: body(): later.append(lax.ppermute(later[-1], 'tensor', down))]
    all_gather x1 -> x0, waiting for transfers between devices: 57.4 us -> none  [body(): lax.all_gather(grad_result.astype(jnp.bfloat16), 'tensor', axis=0, tiled=...]
    all_gather x1, waiting for transfers between devices: 65.5 us -> 10.5 us  [body(): second_all = lax.all_gather(second_low, 'tensor', axis=0, tiled=True)]
    all_gather x1, waiting for transfers between devices: 27.3 us -> 0.01 us  [body(): lax.all_gather(w_up, 'dp', axis=0, tiled=True)]
  transfers between devices with their start and end apart: 20 -> 22, of which waited for: 19 -> 20; matrix products, arithmetic and copies ran while one was open for 12% -> 14% of each run, Pallas kernels for 0% -> 0%
where the time goes in v1:
time: 1130 us; the launch traced here: 1120 us
  waiting for transfers between devices  820 us (73%)
  matrix products  132 us (12%)
  blocking collectives  75.5 us (7%)
  other arithmetic  49.3 us (4%)
  local copies, waits for them, and re-layouts  23.1 us (2%)
  between operations  16.7 us (1%)
    reduce_scatter x1, waiting for transfers between devices, body(): lax.psum_scatter(jnp.dot(attended, out_full, preferred_element_type=jnp.f...  110 us
    reduce_scatter x1, waiting for transfers between devices, body(): lax.psum_scatter(transposed(grad_gate_low, gate_full) + transposed(grad_u...  103 us
    reduce_scatter x1, waiting for transfers between devices, body(): lax.psum_scatter(jnp.dot(hidden, down_full, preferred_element_type=jnp.fl...  61.2 us
    reduce_scatter x1, waiting for transfers between devices, body(): lax.psum_scatter((transposed(grad_query_proj, query_full) + transposed(gr...  61.1 us
    reduce_scatter x1, waiting for transfers between devices, body(): lax.psum_scatter(grad_gate_w.astype(jnp.bfloat16), 'dp', scatter_dimensio...  47.4 us
    psum x1, blocking collectives, body(): lax.psum((first_gain_part, second_gain_part), ('dp', 'tensor'))  40.3 us
    all_gather x1, waiting for transfers between devices, body(): lax.all_gather(grad_middle.astype(jnp.bfloat16), 'tensor', axis=0, tiled=...  39.7 us
    all_gather x1, waiting for transfers between devices, body(): first_all = lax.all_gather(first_low, 'tensor', axis=0, tiled=True)  39.4 us
  transfers between devices with their start and end apart: 22, of which 20 were waited for; matrix products, arithmetic and copies ran while one was open for 14% of the time, Pallas kernels for 0%

profile of v1, /device:TPU:0, one launch (start us, length us, event | category | flops | bytes accessed | tf_op | source)
XLA Modules:
  0.0 1123.4 jit_solution(12158879838844376301)
XLA Ops:
  12.3 15.5 %all-reduce.5 = (bf16[1536]{0:T(1024)(128)(2,1)S(1)}, bf16[1536]{0:T(1024)(128)(2,1)S(1)}) all-reduce(bf16[1536]{0:T(1024)(128)(2,1)S(1)} %dynamic-update-slice.10, bf16[1536]{0:T(1024)(128)(2,1)S(1)} %dynamic-update-slice.11), channel_id=1, replica_groups=mesh['dp'=8,'tensor'=4] {'dp'}, use_global_device_ids=true, to_apply=%add.2 | all-reduce | flops 3072 | bytes 12288
  33.5 9.4 all_gather.46
  42.9 10.4 all_gather.45
  53.6 39.4 %all-gather.9.cloned.1.call-done = bf16[1024,1536]{1,0:T(8,128)(2,1)} async-done(((bf16[256,1536]{1,0:T(8,128)(2,1)}), bf16[1024,1536]{1,0:T(8,128)(2,1)}) %all-gather.9.cloned.1.call-update) | async-done | bytes 3145744 | tf_op jit(solution)/shard_map/all_gather | solution.py:109
  98.4 19.2 %all-gather.11.cloned.1.call-done = bf16[1536,384]{1,0:T(8,128)(2,1)} async-done(((bf16[192,384]{1,0:T(8,128)(2,1)}), bf16[1536,384]{1,0:T(8,128)(2,1)}) %all-gather.11.cloned.1.call-update) | async-done | bytes 1179664 | tf_op jit(solution)/shard_map/all_gather | solution.py:96
  132.2 11.2 all-gather.13.cloned.1.call-done
  149.8 110.3 %reduce-scatter.12.cloned.1.call-done = f32[256,1536]{1,0:T(8,128)} async-done(((f32[1024,1536]{1,0:T(8,128)}), f32[256,1536]{1,0:T(8,128)}) %reduce-scatter.12.cloned.1.call-update) | async-done | bytes 1572880 | tf_op jit(solution)/shard_map/reduce_scatter | solution.py:149
  267.5 19.8 %collective-permute-done = bf16[256,1536]{1,0:T(8,128)(2,1)} collective-permute-done((bf16[256,1536]{1,0:T(8,128)(2,1)}, bf16[256,1536]{1,0:T(8,128)(2,1)}, u32[]{:S(2)}, u32[]{:S(2)}) %collective-permute-start) | collective-permute-done | bytes 786464 | tf_op jit(solution)/shard_map/ppermute | solution.py:194
  291.2 19.1 %collective-permute-done.1 = bf16[256,1536]{1,0:T(8,128)(2,1)} collective-permute-done((bf16[256,1536]{1,0:T(8,128)(2,1)}, bf16[256,1536]{1,0:T(8,128)(2,1)}, u32[]{:S(2)}, u32[]{:S(2)}) %collective-permute-start.1) | collective-permute-done | bytes 786464 | tf_op jit(solution)/shard_map/ppermute | solution.py:194
  315.6 39.2 %collective-permute-done.2 = bf16[256,1536]{1,0:T(8,128)(2,1)} collective-permute-done((bf16[256,1536]{1,0:T(8,128)(2,1)}, bf16[256,1536]{1,0:T(8,128)(2,1)}, u32[]{:S(2)}, u32[]{:S(2)}) %collective-permute-start.2) | collective-permute-done | bytes 786464 | tf_op jit(solution)/shard_map/ppermute | solution.py:196
  364.3 10.5 all-gather.15.cloned.1.call-done
  374.8 8.2 fusion.68
  383.0 25.0 %all-gather.17.cloned.1.call-done = bf16[1536,1024]{1,0:T(8,128)(2,1)} async-done(((bf16[192,1024]{1,0:T(8,128)(2,1)}), bf16[1536,1024]{1,0:T(8,128)(2,1)}) %all-gather.17.cloned.1.call-update) | async-done | bytes 3145744 | tf_op jit(solution)/shard_map/all_gather | solution.py:157
  408.0 8.2 fusion.67
  416.2 25.8 %all-gather.21.cloned.1.call-done = bf16[1024,1536]{0,1:T(8,128)(2,1)} async-done(((bf16[1024,192]{0,1:T(8,128)(2,1)}), bf16[1024,1536]{0,1:T(8,128)(2,1)}) %all-gather.21.cloned.1.call-update) | async-done | bytes 3145744 | tf_op jit(solution)/shard_map/all_gather | solution.py:159
  442.1 11.6 %multiply_convert_fusion = (bf16[1024,1024]{1,0:T(8,128)(2,1)S(1)}, bf16[1024,1024]{1,0:T(8,128)(2,1)S(1)}, bf16[1024,1024]{1,0:T(8,128)(2,1)}) fusion(f32[1024,1024]{1,0:T(8,128)} %fusion.67, f32[1024,1024]{1,0:T(8,128)} %fusion.68, bf16[1024,1536]{0,1:T(8,128)(2,1)} %all-gather.21.cloned.1.call-done, ...), kind=kOutput, calls=%fused_computation.18 | convolution fusion | flops 3238002688 | bytes 20971524 | tf_op jit(solution)/shard_map/dot_general | solution.py:43
  463.3 7.7 convolution_convert_fusion.3
  471.0 103.1 %reduce-scatter.16.cloned.1.call-done = f32[256,1536]{1,0:T(8,128)} async-done(((f32[1024,1536]{1,0:T(8,128)}), f32[256,1536]{1,0:T(8,128)}) %reduce-scatter.16.cloned.1.call-update) | async-done | bytes 1572880 | tf_op jit(solution)/shard_map/reduce_scatter | solution.py:205
  576.1 61.2 %reduce-scatter.14.cloned.1.call-done = bf16[256,1536]{1,0:T(8,128)(2,1)} async-done(((bf16[1024,1536]{1,0:T(8,128)(2,1)}), bf16[256,1536]{1,0:T(8,128)(2,1)}) %reduce-scatter.14.cloned.1.call-update) | async-done | bytes 786448 | tf_op jit(solution)/shard_map/reduce_scatter | solution.py:171
  641.8 7.7 convolution_convert_fusion
  649.6 8.0 convolution_convert_fusion.1
  657.7 7.6 convolution_convert_fusion.2
  665.6 39.7 %all-gather.23.cloned.1.call-done = bf16[1024,1536]{1,0:T(8,128)(2,1)} async-done(((bf16[256,1536]{1,0:T(8,128)(2,1)}), bf16[1024,1536]{1,0:T(8,128)(2,1)}) %all-gather.23.cloned.1.call-update) | async-done | bytes 3145744 | tf_op jit(solution)/shard_map/all_gather | solution.py:226
  720.9 9.5 fusion
  766.7 36.1 %reduce-scatter.30.cloned.1.call-done = bf16[192,1024]{1,0:T(8,128)(2,1)} async-done(((bf16[1536,1024]{1,0:T(8,128)(2,1)}), bf16[192,1024]{1,0:T(8,128)(2,1)}) %reduce-scatter.30.cloned.1.call-update) | async-done | bytes 393232 | tf_op jit(solution)/shard_map/reduce_scatter | solution.py:217
  804.7 47.4 %reduce-scatter.28.cloned.1.call-done = bf16[192,1024]{1,0:T(8,128)(2,1)} async-done(((bf16[1536,1024]{1,0:T(8,128)(2,1)}), bf16[192,1024]{1,0:T(8,128)(2,1)}) %reduce-scatter.28.cloned.1.call-update) | async-done | bytes 393232 | tf_op jit(solution)/shard_map/reduce_scatter | solution.py:214
  854.0 36.0 %reduce-scatter.24.cloned.1.call-done = bf16[192,192]{1,0:T(8,128)(2,1)} async-done(((bf16[1536,192]{1,0:T(8,128)(2,1)}), bf16[192,192]{1,0:T(8,128)(2,1)}) %reduce-scatter.24.cloned.1.call-update) | async-done | bytes 73744 | tf_op jit(solution)/shard_map/reduce_scatter | solution.py:296
  891.6 36.4 %reduce-scatter.22.cloned.1.call-done = bf16[192,192]{1,0:T(8,128)(2,1)} async-done(((bf16[1536,192]{1,0:T(8,128)(2,1)}), bf16[192,192]{1,0:T(8,128)(2,1)}) %reduce-scatter.22.cloned.1.call-update) | async-done | bytes 73744 | tf_op jit(solution)/shard_map/reduce_scatter | solution.py:293
  929.6 38.2 %reduce-scatter.26.cloned.1.call-done = bf16[384,192]{0,1:T(8,128)(2,1)} async-done(((bf16[384,1536]{0,1:T(8,128)(2,1)}), bf16[384,192]{0,1:T(8,128)(2,1)}) %reduce-scatter.26.cloned.1.call-update) | async-done | bytes 147472 | tf_op jit(solution)/shard_map/reduce_scatter | solution.py:299
  969.4 38.2 %reduce-scatter.20.cloned.1.call-done = bf16[192,384]{1,0:T(8,128)(2,1)} async-done(((bf16[1536,384]{1,0:T(8,128)(2,1)}), bf16[192,384]{1,0:T(8,128)(2,1)}) %reduce-scatter.20.cloned.1.call-update) | async-done | bytes 147472 | tf_op jit(solution)/shard_map/reduce_scatter | solution.py:290
  1009.2 61.1 %reduce-scatter.18.cloned.1.call-done = bf16[256,1536]{1,0:T(8,128)(2,1)} async-done(((bf16[1024,1536]{1,0:T(8,128)(2,1)}), bf16[256,1536]{1,0:T(8,128)(2,1)}) %reduce-scatter.18.cloned.1.call-update) | async-done | bytes 786448 | tf_op jit(solution)/shard_map/reduce_scatter | solution.py:276
  1072.1 40.3 %all-reduce.4 = (f32[1536]{0:T(1024)S(1)}, f32[1536]{0:T(1024)S(1)}) all-reduce(f32[1536]{0:T(1024)S(1)} %get-tuple-element.77, f32[1536]{0:T(1024)S(1)} %get-tuple-element.75), channel_id=1, replica_groups=mesh['dp'=8,'tensor'=4] {'dp','tensor'}, use_global_device_ids=true, to_apply=%region_15.16 | all-reduce | flops 3072 | bytes 24576 | tf_op jit(solution)/shard_map/psum | solution.py:305
  (237 shorter events, 145.7 us)
Async XLA Ops:
  7.2 85.8 %all-gather.9.cloned.1.call-start = ((), (), s32[]{:S(2)}) async-start(), calls=%async_computation.11 | async-start | bytes 3932160 | tf_op jit(solution)/shard_map/all_gather | solution.py:109
  30.1 87.4 %all-gather.11.cloned.1.call-start = ((), (), s32[]{:S(2)}) async-start(), calls=%async_computation.12 | async-start | bytes 1327104 | tf_op jit(solution)/shard_map/all_gather | solution.py:96
  30.8 112.5 %all-gather.13.cloned.1.call-start = ((), (), s32[]{:S(2)}) async-start(), calls=%async_computation.13 | async-start | bytes 1327104 | tf_op jit(solution)/shard_map/all_gather | solution.py:99
  31.6 228.5 %reduce-scatter.12.cloned.1.call-start = ((), (), s32[]{:S(2)}) async-start(), calls=%async_computation.14 | async-start | bytes 7864320 | tf_op jit(solution)/shard_map/reduce_scatter | solution.py:149
  33.1 88.1 %copy-start.17 = (f32[1024,48]{0,1:T(8,128)}, f32[1024,48]{0,1:T(8,128)S(1)}, u32[]{:S(2)}) copy-start(f32[1024,48]{0,1:T(8,128)S(1)} %get-tuple-element.103) | copy-start | bytes 589828
  33.1 88.1 %copy-start.19 = (f32[1024,48]{0,1:T(8,128)}, f32[1024,48]{0,1:T(8,128)S(1)}, u32[]{:S(2)}) copy-start(f32[1024,48]{0,1:T(8,128)S(1)} %get-tuple-element.104) | copy-start | bytes 589828
  42.9 55.3 %copy-start.12 = (bf16[1536,192]{1,0:T(8,128)(2,1)}, bf16[1536,192]{1,0:T(8,128)(2,1)S(1)}, u32[]{:S(2)}) copy-start(bf16[1536,192]{1,0:T(8,128)(2,1)S(1)} %all_gather.46) | copy-start | bytes 1769476
  53.3 44.9 %copy-start.10 = (bf16[1536,192]{1,0:T(8,128)(2,1)}, bf16[1536,192]{1,0:T(8,128)(2,1)S(1)}, u32[]{:S(2)}) copy-start(bf16[1536,192]{1,0:T(8,128)(2,1)S(1)} %all_gather.45) | copy-start | bytes 1769476
  53.6 655.2 %copy-start.14 = (pred[512,512]{0,1:T(8,128)(4,1)}, pred[512,512]{0,1:T(8,128)(4,1)S(1)}, u32[]{:S(2)}) copy-start(pred[512,512]{0,1:T(8,128)(4,1)S(1)} %fusion.35) | copy-start | bytes 786436
  149.1 111.0 %copy-start.4 = (bf16[1,256,1536]{2,1,0:T(8,128)(2,1)S(1)}, bf16[1,256,1536]{2,1,0:T(8,128)(2,1)}, u32[]{:S(2)}) copy-start(bf16[1,256,1536]{2,1,0:T(8,128)(2,1)} %param.24) | copy-start | bytes 2359300
  149.1 215.1 %all-gather.19.cloned.1.call-start = ((), (), s32[]{:S(2)}) async-start(), calls=%async_computation.17 | async-start | bytes 3538944 | tf_op jit(solution)/shard_map/all_gather | solution.py:158
  149.7 225.1 %all-gather.15.cloned.1.call-start = ((), (), s32[]{:S(2)}) async-start(), calls=%async_computation.15 | async-start | bytes 3932160 | tf_op jit(solution)/shard_map/all_gather | solution.py:166
  262.9 145.1 %all-gather.17.cloned.1.call-start = ((), (), s32[]{:S(2)}) async-start(), calls=%async_computation.16 | async-start | bytes 3538944 | tf_op jit(solution)/shard_map/all_gather | solution.py:157
  263.6 178.5 %all-gather.21.cloned.1.call-start = ((), (), s32[]{:S(2)}) async-start(), calls=%async_computation.18 | async-start | bytes 3538944 | tf_op jit(solution)/shard_map/all_gather | solution.py:159
  265.9 21.3 %collective-permute-start = (bf16[256,1536]{1,0:T(8,128)(2,1)}, bf16[256,1536]{1,0:T(8,128)(2,1)}, u32[]{:S(2)}, u32[]{:S(2)}) collective-permute-start(bf16[256,1536]{1,0:T(8,128)(2,1)} %fusion.27), channel_id=1, source_target_pairs={{0,1},{1,2},{2,3},{3,0},{4,5},{5,6},{6,7},{7,4},{8,9},{9,10},{10,1... | collective-permute-start | bytes 2359304 | tf_op jit(solution)/shard_map/ppermute | solution.py:194
  267.4 306.8 %reduce-scatter.16.cloned.1.call-start = ((), (), s32[]{:S(2)}) async-start(), calls=%async_computation.20 | async-start | bytes 7864320 | tf_op jit(solution)/shard_map/reduce_scatter | solution.py:205
  287.3 23.1 %collective-permute-start.1 = (bf16[256,1536]{1,0:T(8,128)(2,1)}, bf16[256,1536]{1,0:T(8,128)(2,1)}, u32[]{:S(2)}, u32[]{:S(2)}) collective-permute-start(bf16[256,1536]{1,0:T(8,128)(2,1)} %collective-permute-done), channel_id=1, source_target_pairs={{0,1},{1,2},{2,3},{3,0},{4,5},{5,6},{6,7},{7,4},{8,9},{9,10},{10,1... | collective-permute-start | bytes 2359304 | tf_op jit(solution)/shard_map/ppermute | solution.py:194
  287.3 67.6 %collective-permute-start.2 = (bf16[256,1536]{1,0:T(8,128)(2,1)}, bf16[256,1536]{1,0:T(8,128)(2,1)}, u32[]{:S(2)}, u32[]{:S(2)}) collective-permute-start(bf16[256,1536]{1,0:T(8,128)(2,1)} %fusion.27), channel_id=1, source_target_pairs={{0,3},{1,0},{2,1},{3,2},{4,7},{5,4},{6,5},{7,6},{8,11},{9,8},{10,9... | collective-permute-start | bytes 2359304 | tf_op jit(solution)/shard_map/ppermute | solution.py:196
  463.3 174.0 %reduce-scatter.14.cloned.1.call-start = ((), (), s32[]{:S(2)}) async-start(), calls=%async_computation.19 | async-start | bytes 3932160 | tf_op jit(solution)/shard_map/reduce_scatter | solution.py:171
  471.0 234.3 %all-gather.23.cloned.1.call-start = ((), (), s32[]{:S(2)}) async-start(), calls=%async_computation.21 | async-start | bytes 3932160 | tf_op jit(solution)/shard_map/all_gather | solution.py:226
  641.8 122.8 %reduce-scatter.32.cloned.1.call-start = ((), (), s32[]{:S(2)}) async-start(), calls=%async_computation.29 | async-start | bytes 3538944 | tf_op jit(solution)/shard_map/reduce_scatter | solution.py:220
  649.5 153.2 %reduce-scatter.30.cloned.1.call-start = ((), (), s32[]{:S(2)}) async-start(), calls=%async_computation.28 | async-start | bytes 3538944 | tf_op jit(solution)/shard_map/reduce_scatter | solution.py:217
  657.6 194.4 %reduce-scatter.28.cloned.1.call-start = ((), (), s32[]{:S(2)}) async-start(), calls=%async_computation.27 | async-start | bytes 3538944 | tf_op jit(solution)/shard_map/reduce_scatter | solution.py:214
  665.3 39.9 %copy-start.35 = (bf16[384,1536]{0,1:T(8,128)(2,1)S(1)}, bf16[384,1536]{0,1:T(8,128)(2,1)}, u32[]{:S(2)}) copy-start(bf16[384,1536]{0,1:T(8,128)(2,1)} %all-gather.13.cloned.1.call-done) | copy-start | bytes 3538948
  665.4 224.7 %reduce-scatter.24.cloned.1.call-start = ((), (), s32[]{:S(2)}) async-start(), calls=%async_computation.25 | async-start | bytes 884736 | tf_op jit(solution)/shard_map/reduce_scatter | solution.py:296
  730.5 197.5 %reduce-scatter.22.cloned.1.call-start = ((), (), s32[]{:S(2)}) async-start(), calls=%async_computation.24 | async-start | bytes 884736 | tf_op jit(solution)/shard_map/reduce_scatter | solution.py:293
  743.7 224.1 %reduce-scatter.26.cloned.1.call-start = ((), (), s32[]{:S(2)}) async-start(), calls=%async_computation.26 | async-start | bytes 1327104 | tf_op jit(solution)/shard_map/reduce_scatter | solution.py:299
  748.9 258.7 %reduce-scatter.20.cloned.1.call-start = ((), (), s32[]{:S(2)}) async-start(), calls=%async_computation.23 | async-start | bytes 1327104 | tf_op jit(solution)/shard_map/reduce_scatter | solution.py:290
  758.2 312.1 %reduce-scatter.18.cloned.1.call-start = ((), (), s32[]{:S(2)}) async-start(), calls=%async_computation.22 | async-start | bytes 3932160 | tf_op jit(solution)/shard_map/reduce_scatter | solution.py:276
  764.5 305.8 %copy-start.42 = (f32[1536]{0:T(1024)S(1)}, f32[1536]{0:T(1024)}, u32[]{:S(2)}) copy-start(f32[1536]{0:T(1024)} %copy-done.41) | copy-start | bytes 18436
  764.5 305.8 %copy-start.46 = (f32[256]{0:T(256)S(1)}, f32[256]{0:T(256)}, u32[]{:S(2)}) copy-start(f32[256]{0:T(256)} %copy-done.45) | copy-start | bytes 3076
  764.5 349.1 %copy-start.16 = (f32[256,1536]{1,0:T(8,128)S(1)}, f32[256,1536]{1,0:T(8,128)}, u32[]{:S(2)}) copy-start(f32[256,1536]{1,0:T(8,128)} %get-tuple-element.84) | copy-start | bytes 4718596
  (43 other events, 349.2 us)
Sparse Core Ops, SparseCore 0:
  30.2 62.7 all-gather.8
  94.9 22.5 all-gather.10
  119.4 23.9 all-gather.12
  149.3 110.7 reduce-scatter.11
  261.8 32.6 all-gather.18
  296.5 78.2 all-gather.14
  376.7 31.2 all-gather.16
  409.9 32.1 all-gather.20
  463.4 110.7 reduce-scatter.15
  576.3 60.9 reduce-scatter.13
  641.9 63.3 all-gather.22
  708.5 44.6 reduce-scatter.31
  756.6 46.0 reduce-scatter.29
  806.0 46.0 reduce-scatter.27
  855.1 34.9 reduce-scatter.23
  893.0 34.9 reduce-scatter.21
  931.1 36.6 reduce-scatter.25
  970.9 36.6 reduce-scatter.19
  1009.9 60.3 reduce-scatter.17
